TPU v7x, 256 devices: a whole 4x4x8 slice. The times are simulated.
256 devices in a mesh: dp: 32 (over x_lo, z, core), mp: 8 (over x_hi, y).
Axes of the slice: x: 4 (x_hi: 2, x_lo: 2; x = x_hi * 2 + x_lo), y: 4, z: 8, core: 2. Of those that a mesh axis runs over, the one named last changes fastest.
Arguments:
- token_ids: int32 [32, 512], P('dp', 'mp'), may hold values from 0 to 128255
- embedding: bfloat16 [128256, 8192], P('mp', 'dp'), may hold values from -6 to 6
- norm_gain: bfloat16 [8192], replicated, may hold values from 0.099609375 to 1.8984375
- query_weight: bfloat16 [8192, 4096], P('dp', 'mp'), may hold values from -4 to 4
- key_weight: bfloat16 [8192, 1024], P('dp', 'mp'), may hold values from -0.0625 to 0.0625
- value_weight: bfloat16 [8192, 1024], P('dp', 'mp'), may hold values from -0.0625 to 0.0625
Outputs:
- attention: bfloat16 [16384, 4096], P('dp', 'mp')
All inputs are finite; a program needn't handle non-finite values.
Results may differ from a plain program's by a relative error of at most 0.0095.
The roundings to bfloat16 on the way count: a program that leaves them out, or rounds other values in their place, can miss the bound.
Values may be sent and summed in bfloat16 or wider, within the bound.
No kernel may reach another device: no remote copies, remote signals or barrier semaphores. Data moves between devices by JAX's collectives and lax.ppermute only.
A program may use at most 128 MiB of HBM per device.

v0:
```python
import jax
import jax.numpy as jnp
from jax import lax
from jax.sharding import Mesh
from jax.sharding import PartitionSpec as P

HD = 128
MP = ("mp_0", "mp_1")
DP_MP = ("dp", "mp_0", "mp_1")
rope_base = 500000.0
epsilon = 1e-05


def reduced_to_own(tiles, axes, order):
    shape = [lax.axis_size(a) for a in axes]
    tiles = tiles.reshape(*shape, *tiles.shape[1:])
    tiles = tiles.transpose(*order, *range(len(axes), tiles.ndim))
    tiles = tiles.reshape(-1, *tiles.shape[len(axes) :])
    for k in order:
        tiles = lax.psum_scatter(tiles, axes[k], scatter_dimension=0, tiled=True)
    return tiles[0]


def in_blocks(array, dim, size):
    shape = array.shape
    tiles = array.reshape(*shape[:dim], size, shape[dim] // size, *shape[dim + 1 :])
    return jnp.moveaxis(tiles, dim, 0)


def scatter_axes(array, axes, order, dim):
    size = lax.axis_size(axes)
    return reduced_to_own(in_blocks(array, dim, size), axes, order)


def side_by_side(arrays, axis, dim, along):
    both = jnp.concatenate(arrays, axis=along)
    whole, at, outs = (lax.all_gather(both, axis, axis=dim, tiled=True), 0, [])
    for a in arrays:
        outs.append(lax.slice_in_dim(whole, at, at + a.shape[along], axis=along))
        at += a.shape[along]
    return tuple(outs)


def normalize(values, norm_gain):
    factor = lax.rsqrt(jnp.mean(values * values, axis=-1, keepdims=True) + epsilon)
    return (values * factor * norm_gain.astype(jnp.float32)).astype(jnp.bfloat16)


def rotate(values, positions):
    half_width = values.shape[-1] // 2
    frequency = rope_base ** (-(jnp.arange(half_width, dtype=jnp.float32) * 2.0) / values.shape[-1])
    angles = (positions[:, None] * frequency[None, :])[:, None, :]
    cosine = jnp.cos(angles)
    sine_wave = jnp.sin(angles)
    first_half = values[..., :half_width]
    second_half = values[..., half_width:]
    return jnp.concatenate(
        [
            first_half * cosine - second_half * sine_wave,
            second_half * cosine + first_half * sine_wave,
        ],
        axis=-1,
    )


def attend(queries, key_block, value_block):
    length = queries.shape[0]
    scores = jnp.einsum(
        "skgd,tkd->kgst", queries, key_block, preferred_element_type=jnp.float32
    ) * queries.shape[-1] ** (-0.5)
    causal = jnp.arange(length)[:, None] >= jnp.arange(length)[None, :]
    scores = jnp.where(causal, scores, -jnp.inf)
    highest = jnp.max(scores, axis=-1, keepdims=True)
    raised = jnp.exp(scores - highest)
    weights = (raised / jnp.sum(raised, axis=-1, keepdims=True)).astype(jnp.bfloat16)
    blended = jnp.einsum("kgst,tkd->skgd", weights, value_block, preferred_element_type=jnp.float32)
    return blended.reshape(length, -1).astype(jnp.bfloat16)


def per_device(token_ids, embedding, norm_gain, query_weight, key_weight, value_weight):
    responses, span = token_ids.shape
    vocab_rows = embedding.shape[0]
    dp_count = lax.axis_size("dp")
    mp_count = lax.axis_size(MP)
    length = span * mp_count
    flat_ids = token_ids.reshape(responses * span)
    every_id = lax.all_gather(flat_ids, DP_MP, axis=0, tiled=True)
    ordered = every_id.reshape(dp_count, mp_count, responses, span).transpose(0, 2, 1, 3)
    local_ids = ordered - lax.axis_index(MP) * vocab_rows
    inside = (local_ids >= 0) & (local_ids < vocab_rows)
    looked = jnp.take(embedding, jnp.clip(local_ids, 0, vocab_rows - 1), axis=0)
    looked = jnp.where(inside[..., None], looked, jnp.zeros((), jnp.bfloat16))
    shared = scatter_axes(looked, MP, (1, 0), 2).astype(jnp.float32)
    moved = lax.all_to_all(
        shared.astype(jnp.bfloat16), "dp", split_axis=0, concat_axis=4, tiled=True
    )
    share_normed = normalize(moved.astype(jnp.float32).reshape(responses, span, -1), norm_gain)
    normed = lax.all_gather(share_normed, MP, axis=1, tiled=True)
    flat_normed = normed.reshape(responses * length, -1)

    def project(piece):
        return jnp.dot(flat_normed, piece, preferred_element_type=jnp.float32)

    pieces = side_by_side((query_weight, key_weight, value_weight), "dp", 0, 1)
    query_proj = project(pieces[0])
    key_proj = project(pieces[1])
    value_proj = project(pieces[2])
    heads_here = query_weight.shape[1] // HD
    kv_here = key_weight.shape[1] // HD
    positions = jnp.arange(length, dtype=jnp.float32)
    queries = rotate(query_proj.reshape(responses, length, heads_here, HD), positions).astype(
        jnp.bfloat16
    )
    queries = queries.reshape(responses, length, kv_here, heads_here // kv_here, HD)
    key_block = rotate(key_proj.reshape(responses, length, kv_here, HD), positions).astype(
        jnp.bfloat16
    )
    value_block = value_proj.reshape(responses, length, kv_here, HD).astype(jnp.bfloat16)
    output = lax.map(
        lambda group: attend(group[0], group[1], group[2]), (queries, key_block, value_block)
    )
    return output.reshape(responses * length, heads_here * HD)


def solution(mesh):
    split = Mesh(mesh.devices.reshape(mesh.shape["dp"], 2, 4), ("dp", "mp_0", "mp_1"))
    in_specs = (P("dp", MP), P(MP, "dp"), P(), P("dp", MP), P("dp", MP), P("dp", MP))
    out_specs = P("dp", MP)
    return jax.shard_map(
        per_device, mesh=split, in_specs=in_specs, out_specs=out_specs, check_vma=False
    )
```

profile of v0, /device:TPU:1, one launch (start us, length us, event | category | flops | bytes accessed | tf_op | source)
XLA Modules:
  0.0 695.4 jit_solution(9805546646398294829)
XLA Ops:
  7.4 0.8 bitcast_dynamic-update-slice_fusion
  8.1 0.6 copy-done.3
  8.9 250.5 %all-reduce.3.cloned.1.call-done = s32[16384]{0:T(1024)} async-done(((s32[16384]{0:T(1024)}), s32[16384]{0:T(1024)}) %all-reduce.3.cloned.1.call-update) | async-done | bytes 65552
  259.3 0.9 subtract_clamp_fusion
  260.5 0.9 compare_and_fusion.1
  261.5 65.6 %gather_fusion = bf16[16384,256]{1,0:T(8,128)(2,1)} fusion(bf16[16032,256]{1,0:T(8,128)(2,1)} %param.7, s32[16384]{0:T(1024)S(1)} %broadcast_clamp_fusion), kind=kCustom, calls=%fused_computation | custom fusion | bytes 16842752 | tf_op jit(solution)/shard_map/jit(_take)/gather | solution.py:91
  327.1 7.7 %select_select_fusion = bf16[32,1,8,1,64,256]{5,4,2,0,3,1:T(8,128)(2,1)} fusion(bf16[32,1,8,1,64,256]{5,4,2,0,3,1:T(8,128)(2,1)} %bitcast.88, pred[32,8,64]{2,1,0:T(8,128)(4,1)S(1)} %compare_and_fusion, pred[32,8,64]{2,1,0:T(8,128)(4,1)S(1)} %and.23), kind=kLoop, calls=%fused_computation.8 | loop fusion | flops 8388608 | bytes 16809984 | tf_op jit(solution)/shard_map/jit(_where)/select_n | solution.py:92
  334.8 8.3 %copy.19 = bf16[2,4,32,1,1,64,256]{6,5,2,0,1,4,3:T(8,128)(2,1)} copy(bf16[2,4,32,1,1,64,256]{6,5,1,0,2,4,3:T(8,128)(2,1)} %bitcast.90) | data formatting | bytes 16777216 | tf_op jit(solution)/shard_map/reshape | solution.py:16
  343.2 79.3 %reduce-scatter.3.cloned.1.call-done = bf16[2,32,1,1,64,256]{5,4,1,3,2,0:T(8,128)(2,1)} async-done(((bf16[8,32,1,1,64,256]{5,4,1,3,2,0:T(8,128)(2,1)}), bf16[2,32,1,1,64,256]{5,4,1,3,2,0:T(8,128)(2,1)}) %reduce-scatter.3.cloned.1.call-update) | async-done | bytes 2097168 | tf_op jit(solution)/shard_map/reduce_scatter | solution.py:20
  422.6 0.8 pad_maximum_fusion
  423.4 39.8 %reduce-scatter.5.cloned.1.call-done = bf16[1,32,1,1,64,256]{5,4,1,3,2,0:T(8,128)(2,1)} async-done(((bf16[2,32,1,1,64,256]{5,4,1,3,2,0:T(8,128)(2,1)}), bf16[1,32,1,1,64,256]{5,4,1,3,2,0:T(8,128)(2,1)}) %reduce-scatter.5.cloned.1.call-update) | async-done | bytes 1048592 | tf_op jit(solution)/shard_map/reduce_scatter | solution.py:20
  463.1 8.0 %all-to-all-start = ((bf16[32,1,1,64,256]{4,3,2,1,0:T(8,128)(2,1)}), bf16[32,1,1,64,256]{4,3,2,1,0:T(8,128)(2,1)S(1)}, u32[]{:S(2)}, u32[]{:S(2)}) async-start(bf16[32,1,1,64,256]{4,3,2,1,0:T(8,128)(2,1)} %bitcast.92), calls=%async_computation.2 | async-start | bytes 2097152 | tf_op jit(solution)/shard_map/all_to_all | solution.py:94
  471.1 0.2 all-gather.4.cloned.1.call-start
  471.4 37.2 %all-to-all-done = bf16[32,1,1,64,256]{4,3,2,1,0:T(8,128)(2,1)S(1)} async-done(((bf16[32,1,1,64,256]{4,3,2,1,0:T(8,128)(2,1)}), bf16[32,1,1,64,256]{4,3,2,1,0:T(8,128)(2,1)S(1)}, u32[]{:S(2)}, u32[]{:S(2)}) %all-to-all-start) | async-done | bytes 1048608 | tf_op jit(solution)/shard_map/all_to_all | solution.py:94
  508.6 0.3 convert_bitcast_fusion
  508.9 2.5 copy.20
  511.5 1.8 reshape.366
  513.2 0.3 fusion.8
  513.5 1.3 multiply_convert_fusion
  514.9 0.5 fusion.48
  515.5 31.8 %all-gather.6.cloned.1.call-done = bf16[8192,768]{1,0:T(8,128)(2,1)} async-done(((bf16[256,768]{1,0:T(8,128)(2,1)}), bf16[8192,768]{1,0:T(8,128)(2,1)}) %all-gather.6.cloned.1.call-update) | async-done | bytes 12582928 | tf_op jit(solution)/shard_map/all_gather | solution.py:37
  547.2 7.4 %slice_bitcast_fusion = bf16[512,8192]{0,1:T(8,128)(2,1)} fusion(bf16[8192,768]{1,0:T(8,128)(2,1)} %all-gather.6.cloned.1.call-done), kind=kLoop, calls=%fused_computation.1 | loop fusion | bytes 16777216 | tf_op jit(solution)/shard_map/dot_general | solution.py:102
  554.6 12.0 %copy.21 = bf16[512,8192]{1,0:T(8,128)(2,1)} copy(bf16[512,8192]{0,1:T(8,128)(2,1)} %slice_bitcast_fusion) | data formatting | bytes 16777216 | tf_op jit(solution)/shard_map/dot_general | solution.py:102
  566.6 93.0 %all-gather.4.cloned.1.call-done = bf16[1,512,8192]{2,1,0:T(8,128)(2,1)} async-done(((bf16[1,64,8192]{2,1,0:T(8,128)(2,1)}), bf16[1,512,8192]{2,1,0:T(8,128)(2,1)}) %all-gather.4.cloned.1.call-update) | async-done | bytes 8388624 | tf_op jit(solution)/shard_map/all_gather | solution.py:98
  659.5 7.0 %fusion.20 = f32[1,512,1,128]{1,3,2,0:T(8,128)S(1)} fusion(bf16[8192,768]{1,0:T(8,128)(2,1)} %all-gather.6.cloned.1.call-done, bf16[1,512,8192]{2,1,0:T(8,128)(2,1)} %all-gather.4.cloned.1.call-done), kind=kOutput, calls=%fused_computation.25 | convolution fusion | flops 1073741824 | bytes 10747904 | tf_op jit(solution)/shard_map/dot_general | solution.py:102
  666.6 0.6 fusion.51
  667.1 7.2 %fusion.14 = f32[1,512,4,128]{1,3,2,0:T(8,128)S(1)} fusion(bf16[4,128,8192]{2,1,0:T(8,128)(2,1)} %bitcast.91, bf16[1,512,8192]{2,1,0:T(8,128)(2,1)S(1)} %copy-done), kind=kOutput, calls=%fused_computation.23 | convolution fusion | flops 4294967296 | bytes 17825792 | tf_op jit(solution)/shard_map/dot_general | solution.py:102
  674.5 0.9 fusion.7
  675.4 2.0 copy-done.1
  677.4 0.9 fusion.6
  678.3 9.0 %fusion.17 = bf16[128,4,512]{2,0,1:T(8,128)(2,1)S(1)} fusion(f32[4,512]{1,0:T(4,128)S(1)} %fusion.6, f32[4,512]{1,0:T(4,128)S(1)} %get-tuple-element.26, f32[512,512,4]{1,0,2:T(8,128)} %copy-done.1, pred[512,512]{0,1:T(8,128)(4,1)S(1)} %iota_compare_fusion, bf16[8192,768]{1,0:T(8,128)(2,1)} %all-gather.6.cloned.1.call-done, ...), kind=kOutput, calls=%fused_computation.24 | convolution fusion | flops 1347747840 | bytes 15482880 | tf_op jit(solution)/shard_map/while/body/eval_jaxpr/kgst,tkd->skgd/dot_general | solution.py:76
  687.2 1.0 copy.26
  (34 shorter events, 0.9 us)
Async XLA Ops:
  7.4 251.9 %all-reduce.3.cloned.1.call-start = ((), (), s32[]{:S(2)}) async-start(), calls=%async_computation.7 | async-start | bytes 131072
  8.1 0.6 copy-start.3
  8.8 413.7 %reduce-scatter.3.cloned.1.call-start = ((), (), s32[]{:S(2)}) async-start(), calls=%async_computation.3 | async-start | bytes 10485760 | tf_op jit(solution)/shard_map/reduce_scatter | solution.py:20
  343.1 79.5 %copy-start.2 = (bf16[256,512]{1,0:T(8,128)(2,1)S(1)}, bf16[256,512]{1,0:T(8,128)(2,1)}, u32[]{:S(2)}) copy-start(bf16[256,512]{1,0:T(8,128)(2,1)} %param.9) | copy-start | bytes 786436
  343.1 79.5 %copy-start.4 = (bf16[256,128]{1,0:T(8,128)(2,1)S(1)}, bf16[256,128]{1,0:T(8,128)(2,1)}, u32[]{:S(2)}) copy-start(bf16[256,128]{1,0:T(8,128)(2,1)} %param.11) | copy-start | bytes 196612
  343.1 79.5 %copy-start.5 = (bf16[256,128]{1,0:T(8,128)(2,1)S(1)}, bf16[256,128]{1,0:T(8,128)(2,1)}, u32[]{:S(2)}) copy-start(bf16[256,128]{1,0:T(8,128)(2,1)} %param.10) | copy-start | bytes 196612
  343.1 128.3 %copy-start.6 = (bf16[8192]{0:T(1024)(128)(2,1)S(1)}, bf16[8192]{0:T(1024)(128)(2,1)}, u32[]{:S(2)}) copy-start(bf16[8192]{0:T(1024)(128)(2,1)} %param.8) | copy-start | bytes 49156
  343.1 120.0 %reduce-scatter.5.cloned.1.call-start = ((), (), s32[]{:S(2)}) async-start(), calls=%async_computation.4 | async-start | bytes 3145728 | tf_op jit(solution)/shard_map/reduce_scatter | solution.py:20
  422.5 124.7 %all-gather.6.cloned.1.call-start = ((), (), s32[]{:S(2)}) async-start(), calls=%async_computation.6 | async-start | bytes 12976128 | tf_op jit(solution)/shard_map/all_gather | solution.py:37
  463.1 45.5 %all-to-all-start = ((bf16[32,1,1,64,256]{4,3,2,1,0:T(8,128)(2,1)}), bf16[32,1,1,64,256]{4,3,2,1,0:T(8,128)(2,1)S(1)}, u32[]{:S(2)}, u32[]{:S(2)}) async-start(bf16[32,1,1,64,256]{4,3,2,1,0:T(8,128)(2,1)} %bitcast.92), calls=%async_computation.2 | async-start | bytes 2097152 | tf_op jit(solution)/shard_map/all_to_all | solution.py:94
  471.1 188.4 %all-gather.4.cloned.1.call-start = ((), (), s32[]{:S(2)}) async-start(), calls=%async_computation.5 | async-start | bytes 9437184 | tf_op jit(solution)/shard_map/all_gather | solution.py:98
  659.5 7.6 %copy-start = (bf16[1,512,8192]{2,1,0:T(8,128)(2,1)S(1)}, bf16[1,512,8192]{2,1,0:T(8,128)(2,1)}, u32[]{:S(2)}) copy-start(bf16[1,512,8192]{2,1,0:T(8,128)(2,1)} %all-gather.4.cloned.1.call-done) | copy-start | bytes 25165828
  675.4 2.0 copy-start.1
Sparse Core Ops, SparseCore 0:
  13.7 245.6 all-reduce.2
  343.2 79.1 reduce-scatter.2
  425.0 38.1 reduce-scatter.4
Sparse Core Ops, SparseCore 1:
  424.8 122.3 all-gather.5
  549.7 109.7 all-gather.3
where the time goes:
time: 696 us; the launch traced here: 695 us
  waiting for transfers between devices  532 us (76%)
  local copies, waits for them, and re-layouts  102 us (15%)
  matrix products  24 us (3%)
  between operations  14.8 us (2%)
  other arithmetic  14.3 us (2%)
  starting transfers between devices  8.37 us (1%)
    unnamed x6, waiting for transfers between devices  251 us
    reduce_scatter x2, waiting for transfers between devices, reduced_to_own(): tiles = lax.psum_scatter(tiles, axes[k], scatter_dimension=0, tiled=True)  119 us
    all_gather x1, waiting for transfers between devices, per_device(): normed = lax.all_gather(share_normed, MP, axis=1, tiled=True)  93 us
    gather x1, local copies, waits for them, and re-layouts, per_device(): looked = jnp.take(embedding, jnp.clip(local_ids, 0, vocab_rows - 1), axis=0)  65.6 us
    all_to_all x1, waiting for transfers between devices, per_device(): lax.all_to_all(shared.astype(jnp.bfloat16), 'dp', split_axis=0, concat_ax...  37.2 us
    all_gather x1, waiting for transfers between devices, side_by_side(): whole, at, outs = (lax.all_gather(both, axis, axis=dim, tiled=True), 0, [])  31.8 us
    dot_general x2, local copies, waits for them, and re-layouts, project(): return jnp.dot(flat_normed, piece, preferred_element_type=jnp.float32)  19.4 us
    dot_general x2, matrix products, project(): return jnp.dot(flat_normed, piece, preferred_element_type=jnp.float32)  14.2 us
  transfers between devices with their start and end apart: 6, of which 6 were waited for; matrix products, arithmetic and copies ran while one was open for 4% of the time, Pallas kernels for 0%

commit v1 on v0

--- a/solution.py
+++ b/solution.py
@@ -95,7 +95,10 @@
         shared.astype(jnp.bfloat16), "dp", split_axis=0, concat_axis=4, tiled=True
     )
     share_normed = normalize(moved.astype(jnp.float32).reshape(responses, span, -1), norm_gain)
-    normed = lax.all_gather(share_normed, MP, axis=1, tiled=True)
+    count = lax.axis_size(MP)
+    blocks = jnp.stack([share_normed for _ in range(count)])
+    blocks = lax.all_to_all(blocks, MP, split_axis=0, concat_axis=0)
+    normed = jnp.concatenate(blocks, axis=1)
     flat_normed = normed.reshape(responses * length, -1)
 
     def project(piece):

time: 696 us -> 670 us (0.963)
  waiting for transfers between devices: 532 us -> 503 us
    all_gather x1 -> x0, waiting for transfers between devices: 93 us -> none  [per_device(): normed = lax.all_gather(share_normed, MP, axis=1, tiled=True)]
    all_to_all x0 -> x1, waiting for transfers between devices: none -> 47.2 us  [per_device(): blocks = lax.all_to_all(blocks, MP, split_axis=0, concat_axis=0)]
    all_gather x1, waiting for transfers between devices: 31.8 us -> 48.2 us  [side_by_side(): whole, at, outs = (lax.all_gather(both, axis, axis=dim, tiled=True), 0, [])]
    reshape x1 -> x0, local copies, waits for them, and re-layouts: 8.28 us -> none  [reduced_to_own(): tiles = tiles.reshape(*shape, *tiles.shape[1:])]
    transpose x0 -> x1, local copies, waits for them, and re-layouts: none -> 8.27 us  [reduced_to_own(): tiles = tiles.transpose(*order, *range(len(axes), tiles.ndim))]
    unnamed x6 -> x5, waiting for transfers between devices: 251 us -> 251 us
where the time goes in v1:
time: 670 us; the launch traced here: 669 us
  waiting for transfers between devices  503 us (75%)
  local copies, waits for them, and re-layouts  101 us (15%)
  matrix products  23.9 us (4%)
  between operations  14.8 us (2%)
  other arithmetic  13.6 us (2%)
  starting transfers between devices  13.4 us (2%)
    unnamed x5, waiting for transfers between devices  251 us
    reduce_scatter x2, waiting for transfers between devices, reduced_to_own(): tiles = lax.psum_scatter(tiles, axes[k], scatter_dimension=0, tiled=True)  119 us
    gather x1, local copies, waits for them, and re-layouts, per_device(): looked = jnp.take(embedding, jnp.clip(local_ids, 0, vocab_rows - 1), axis=0)  65.3 us
    all_gather x1, waiting for transfers between devices, side_by_side(): whole, at, outs = (lax.all_gather(both, axis, axis=dim, tiled=True), 0, [])  48.2 us
    all_to_all x1, waiting for transfers between devices, per_device(): blocks = lax.all_to_all(blocks, MP, split_axis=0, concat_axis=0)  47.2 us
    all_to_all x1, waiting for transfers between devices, per_device(): lax.all_to_all(shared.astype(jnp.bfloat16), 'dp', split_axis=0, concat_ax...  37.5 us
    dot_general x2, local copies, waits for them, and re-layouts, project(): return jnp.dot(flat_normed, piece, preferred_element_type=jnp.float32)  18.5 us
    dot_general x2, matrix products, project(): return jnp.dot(flat_normed, piece, preferred_element_type=jnp.float32)  14 us
  transfers between devices with their start and end apart: 6, of which 6 were waited for; matrix products, arithmetic and copies ran while one was open for 4% of the time, Pallas kernels for 0%

profile of v1, /device:TPU:1, one launch (start us, length us, event | category | flops | bytes accessed | tf_op | source)
XLA Modules:
  0.0 669.3 jit_solution(4049865172269378951)
XLA Ops:
  7.4 0.8 bitcast_dynamic-update-slice_fusion
  8.1 0.6 copy-done.3
  8.9 250.5 %all-reduce.3.cloned.1.call-done = s32[16384]{0:T(1024)} async-done(((s32[16384]{0:T(1024)}), s32[16384]{0:T(1024)}) %all-reduce.3.cloned.1.call-update) | async-done | bytes 65552
  259.3 0.9 subtract_clamp_fusion
  260.6 0.9 compare_and_fusion.1
  261.5 65.3 %gather_fusion = bf16[16384,256]{1,0:T(8,128)(2,1)} fusion(bf16[16032,256]{1,0:T(8,128)(2,1)} %param.7, s32[16384]{0:T(1024)S(1)} %broadcast_clamp_fusion), kind=kCustom, calls=%fused_computation | custom fusion | bytes 16842752 | tf_op jit(solution)/shard_map/jit(_take)/gather | solution.py:91
  326.8 7.8 %fusion = bf16[32,1,8,1,64,256]{5,4,0,2,3,1:T(8,128)(2,1)} fusion(bf16[32,1,8,1,64,256]{5,4,2,0,3,1:T(8,128)(2,1)} %bitcast.83, pred[32,8,64]{2,0,1:T(8,128)(4,1)S(1)} %copy.38, pred[32,8,64]{2,0,1:T(8,128)(4,1)S(1)} %copy.37), kind=kLoop, calls=%fused_computation.3 | loop fusion | flops 8388608 | bytes 16809984 | tf_op jit(solution)/shard_map/jit(_where)/select_n | solution.py:92
  334.6 8.3 %copy.40 = bf16[4,2,32,1,1,64,256]{6,5,2,1,0,4,3:T(8,128)(2,1)} copy(bf16[4,2,32,1,1,64,256]{6,5,2,0,1,4,3:T(8,128)(2,1)} %bitcast.85) | data formatting | bytes 16777216 | tf_op jit(solution)/shard_map/transpose | solution.py:17
  343.0 79.3 %reduce-scatter.3.cloned.1.call-done = bf16[2,32,1,1,64,256]{5,4,1,0,3,2:T(8,128)(2,1)} async-done(((bf16[8,32,1,1,64,256]{5,4,1,0,3,2:T(8,128)(2,1)}), bf16[2,32,1,1,64,256]{5,4,1,0,3,2:T(8,128)(2,1)}) %reduce-scatter.3.cloned.1.call-update) | async-done | bytes 2097168 | tf_op jit(solution)/shard_map/reduce_scatter | solution.py:20
  422.4 0.8 pad_maximum_fusion
  423.2 39.8 %reduce-scatter.5.cloned.1.call-done = bf16[1,32,1,1,64,256]{5,4,1,0,3,2:T(8,128)(2,1)} async-done(((bf16[2,32,1,1,64,256]{5,4,1,0,3,2:T(8,128)(2,1)}), bf16[1,32,1,1,64,256]{5,4,1,0,3,2:T(8,128)(2,1)}) %reduce-scatter.5.cloned.1.call-update) | async-done | bytes 1048592 | tf_op jit(solution)/shard_map/reduce_scatter | solution.py:20
  463.0 8.0 %all-to-all-start = ((bf16[32,1,1,64,256]{4,3,2,1,0:T(8,128)(2,1)}), bf16[32,1,1,64,256]{4,3,2,1,0:T(8,128)(2,1)S(1)}, u32[]{:S(2)}, u32[]{:S(2)}) async-start(bf16[32,1,1,64,256]{4,3,2,1,0:T(8,128)(2,1)} %bitcast.88), calls=%async_computation.2 | async-start | bytes 2097152 | tf_op jit(solution)/shard_map/all_to_all | solution.py:94
  471.0 37.5 %all-to-all-done = bf16[32,1,1,64,256]{4,3,2,1,0:T(8,128)(2,1)S(1)} async-done(((bf16[32,1,1,64,256]{4,3,2,1,0:T(8,128)(2,1)}), bf16[32,1,1,64,256]{4,3,2,1,0:T(8,128)(2,1)S(1)}, u32[]{:S(2)}, u32[]{:S(2)}) %all-to-all-start) | async-done | bytes 1048608 | tf_op jit(solution)/shard_map/all_to_all | solution.py:94
  508.5 0.3 fusion.42
  508.8 0.2 copy.55
  509.0 0.3 fusion.3
  509.3 0.3 multiply_convert_fusion
  509.6 4.3 stack.2
  513.9 5.2 all-to-all-start.1
  519.2 0.5 fusion.34
  519.7 48.2 %all-gather.3.cloned.1.call-done = bf16[8192,768]{1,0:T(8,128)(2,1)} async-done(((bf16[256,768]{1,0:T(8,128)(2,1)}), bf16[8192,768]{1,0:T(8,128)(2,1)}) %all-gather.3.cloned.1.call-update) | async-done | bytes 12582928 | tf_op jit(solution)/shard_map/all_gather | solution.py:37
  568.0 7.1 %slice_bitcast_fusion = bf16[512,8192]{0,1:T(8,128)(2,1)} fusion(bf16[8192,768]{1,0:T(8,128)(2,1)} %all-gather.3.cloned.1.call-done), kind=kLoop, calls=%fused_computation.1 | loop fusion | bytes 16777216 | tf_op jit(solution)/shard_map/dot_general | solution.py:105
  575.1 11.3 %copy.43 = bf16[512,8192]{1,0:T(8,128)(2,1)} copy(bf16[512,8192]{0,1:T(8,128)(2,1)} %slice_bitcast_fusion) | data formatting | bytes 16777216 | tf_op jit(solution)/shard_map/dot_general | solution.py:105
  586.4 47.2 %all-to-all-done.1 = bf16[8,1,64,8192]{3,2,1,0:T(8,128)(2,1)} async-done(((bf16[8,1,64,8192]{3,2,1,0:T(8,128)(2,1)}), bf16[8,1,64,8192]{3,2,1,0:T(8,128)(2,1)}, u32[]{:S(2)}, u32[]{:S(2)}) %all-to-all-start.1) | async-done | bytes 8388640 | tf_op jit(solution)/shard_map/all_to_all | solution.py:100
  633.6 7.0 %fusion.14 = f32[1,512,1,128]{1,3,2,0:T(8,128)S(1)} fusion(bf16[512,8192]{1,0:T(8,128)(2,1)} %bitcast.10, bf16[8192,768]{1,0:T(8,128)(2,1)} %all-gather.3.cloned.1.call-done), kind=kOutput, calls=%fused_computation.22 | convolution fusion | flops 1073741824 | bytes 10747904 | tf_op jit(solution)/shard_map/dot_general | solution.py:105
  640.7 0.6 fusion.37
  641.2 7.0 %convolution_bitcast_fusion = f32[1,512,4,128]{1,3,2,0:T(8,128)S(1)} fusion(bf16[512,8192,1]{1,0,2:T(8,128)(2,1)} %bitcast.16, bf16[4,128,8192]{2,1,0:T(8,128)(2,1)S(1)} %bitcast.86), kind=kOutput, calls=%fused_computation.20 | convolution fusion | flops 4294967296 | bytes 17825792 | tf_op jit(solution)/shard_map/dot_general | solution.py:105
  648.5 0.9 fusion.2
  649.4 2.0 copy-done.1
  651.3 0.9 fusion.1
  652.2 9.0 %fusion.11 = bf16[128,4,512]{2,0,1:T(8,128)(2,1)S(1)} fusion(f32[4,512]{1,0:T(4,128)S(1)} %fusion.1, f32[4,512]{1,0:T(4,128)S(1)} %get-tuple-element.26, f32[512,512,4]{1,0,2:T(8,128)} %copy-done.1, pred[512,512]{0,1:T(8,128)(4,1)S(1)} %iota_compare_fusion, bf16[512,8192]{1,0:T(8,128)(2,1)} %bitcast.10, bf16[8192,768]{1,0:T(8,128)(2,1)} %all-gather.3.cloned.1.call-done), kind=kOutput, calls=%fused_computation.21 | convolution fusion | flops 1347747840 | bytes 15482880 | tf_op jit(solution)/shard_map/while/body/eval_jaxpr/kgst,tkd->skgd/dot_general | solution.py:76
  661.2 1.0 copy.48
  (35 shorter events, 1.0 us)
Async XLA Ops:
  7.4 251.9 %all-reduce.3.cloned.1.call-start = ((), (), s32[]{:S(2)}) async-start(), calls=%async_computation.7 | async-start | bytes 131072
  8.1 0.6 copy-start.3
  8.8 413.5 %reduce-scatter.3.cloned.1.call-start = ((), (), s32[]{:S(2)}) async-start(), calls=%async_computation.4 | async-start | bytes 10485760 | tf_op jit(solution)/shard_map/reduce_scatter | solution.py:20
  342.9 79.5 %copy-start.2 = (bf16[256,512]{1,0:T(8,128)(2,1)S(1)}, bf16[256,512]{1,0:T(8,128)(2,1)}, u32[]{:S(2)}) copy-start(bf16[256,512]{1,0:T(8,128)(2,1)} %param.9) | copy-start | bytes 786436
  342.9 79.5 %copy-start.4 = (bf16[256,128]{1,0:T(8,128)(2,1)S(1)}, bf16[256,128]{1,0:T(8,128)(2,1)}, u32[]{:S(2)}) copy-start(bf16[256,128]{1,0:T(8,128)(2,1)} %param.11) | copy-start | bytes 196612
  342.9 79.5 %copy-start.5 = (bf16[256,128]{1,0:T(8,128)(2,1)S(1)}, bf16[256,128]{1,0:T(8,128)(2,1)}, u32[]{:S(2)}) copy-start(bf16[256,128]{1,0:T(8,128)(2,1)} %param.10) | copy-start | bytes 196612
  342.9 128.1 %copy-start.6 = (bf16[8192]{0:T(1024)(128)(2,1)S(1)}, bf16[8192]{0:T(1024)(128)(2,1)}, u32[]{:S(2)}) copy-start(bf16[8192]{0:T(1024)(128)(2,1)} %param.8) | copy-start | bytes 49156
  343.0 120.0 %reduce-scatter.5.cloned.1.call-start = ((), (), s32[]{:S(2)}) async-start(), calls=%async_computation.5 | async-start | bytes 3145728 | tf_op jit(solution)/shard_map/reduce_scatter | solution.py:20
  422.3 145.6 %all-gather.3.cloned.1.call-start = ((), (), s32[]{:S(2)}) async-start(), calls=%async_computation.6 | async-start | bytes 12976128 | tf_op jit(solution)/shard_map/all_gather | solution.py:37
  463.0 45.5 %all-to-all-start = ((bf16[32,1,1,64,256]{4,3,2,1,0:T(8,128)(2,1)}), bf16[32,1,1,64,256]{4,3,2,1,0:T(8,128)(2,1)S(1)}, u32[]{:S(2)}, u32[]{:S(2)}) async-start(bf16[32,1,1,64,256]{4,3,2,1,0:T(8,128)(2,1)} %bitcast.88), calls=%async_computation.2 | async-start | bytes 2097152 | tf_op jit(solution)/shard_map/all_to_all | solution.py:94
  513.9 119.8 %all-to-all-start.1 = ((bf16[8,1,64,8192]{3,2,1,0:T(8,128)(2,1)}), bf16[8,1,64,8192]{3,2,1,0:T(8,128)(2,1)}, u32[]{:S(2)}, u32[]{:S(2)}) async-start(bf16[8,1,64,8192]{3,2,1,0:T(8,128)(2,1)} %stack.2), calls=%async_computation.3 | async-start | bytes 16777216 | tf_op jit(solution)/shard_map/all_to_all | solution.py:100
  633.6 7.6 %copy-start = (bf16[512,8192]{1,0:T(8,128)(2,1)S(1)}, bf16[512,8192]{1,0:T(8,128)(2,1)}, u32[]{:S(2)}) copy-start(bf16[512,8192]{1,0:T(8,128)(2,1)} %copy.43) | copy-start | bytes 25165828
  649.3 2.0 copy-start.1
Sparse Core Ops, SparseCore 0:
  13.7 245.6 all-reduce.2
  343.1 79.1 reduce-scatter.2
  424.8 38.1 reduce-scatter.4
Sparse Core Ops, SparseCore 1:
  424.7 143.2 all-gather.2
